TPU v7x, 32 devices: a whole 2x2x4 slice. The times are simulated.
32 devices in a mesh: row: 4 (over y, x), col: 8 (over z, core).
Axes of the slice: x: 2, y: 2, z: 4, core: 2. Of those that a mesh axis runs over, the one named last changes fastest.
Arguments:
- basis: bfloat16 [40, 131072], P(None, ('row', 'col'))
- expand: float32 [3, 8, 40], replicated, may hold values from -1 to 1
- tiles: bfloat16 [3, 3072, 128, 128], P(None, ('row', 'col')), may hold values from -0.3125 to 0.3125
- tile_rows: int32 [3072], P(('row', 'col')), may hold values from 0 to 255, as said below
- tile_cols: int32 [3072], P(('row', 'col')), may hold values from 0 to 127
Outputs:
- new_block: float32 [8, 131072], P(None, ('row', 'col'))
- coefficients: float32 [8, 40], replicated
- factor: float32 [8, 8], replicated
Inputs may be any that keep to these rules, and one draw needn't show every extreme that they name: `tile_rows`: each device's 96 tiles come in 8 runs of 12; the row tiles of run k are 12 distinct values from k * 32 to (k + 1) * 32 - 1.
All inputs are finite; a program needn't handle non-finite values.
Results may differ from a plain program's by a relative error of at most 0.0054.
Values may be sent and summed in bfloat16 or wider, within the bound.
A program may use at most 64 MiB of HBM per device.

v0:
```python
import math
import jax
import jax.numpy as jnp
from jax import lax
from jax.sharding import PartitionSpec as P


def shards(basis, expand, tiles, tile_rows, tile_cols):
    highest = lax.Precision.HIGHEST
    row_count = lax.axis_size("row")
    col_count = lax.axis_size("col")
    krylov, length = basis.shape
    tile_size = tiles.shape[2]
    block_size = expand.shape[1]
    entries = length * row_count * col_count
    inverse_root = 1.0 / math.sqrt(entries)
    region = length // tile_size
    basis_full = basis.astype(jnp.float32)
    series = jnp.einsum("mbk,kn->mbn", expand, basis_full, precision=highest).astype(jnp.bfloat16)
    gathered = lax.all_gather(series, "row", axis=2, tiled=True)
    col_tiles = gathered.reshape(3, block_size, row_count * length // tile_size, tile_size)
    picked = jnp.take(col_tiles, tile_cols, axis=2)
    products = jnp.einsum("mtij,mbtj->bti", tiles, picked, preferred_element_type=jnp.float32)
    slot_count = col_count * region
    onehot = (tile_rows[:, None] == jnp.arange(slot_count, dtype=jnp.int32)[None, :]).astype(
        jnp.float32
    )
    partial_value = jnp.einsum("ts,bti->bsi", onehot, products, precision=highest).reshape(
        block_size, slot_count * tile_size
    )
    applied = lax.psum_scatter(partial_value, "col", scatter_dimension=1, tiled=True)
    raw_proj = jnp.dot(applied, basis_full.T, precision=highest) * inverse_root
    correlation = jnp.dot(basis_full, basis_full.T, precision=highest) / entries
    energy = jnp.dot(applied, applied.T, precision=highest)
    first_pass, correlation, energy = lax.psum((raw_proj, correlation, energy), ("row", "col"))
    second_pass = first_pass - jnp.dot(first_pass, correlation, precision=highest)
    coefficients = first_pass + second_pass
    mixed = jnp.dot(first_pass, coefficients.T, precision=highest)
    curved = jnp.dot(
        jnp.dot(coefficients, correlation, precision=highest), coefficients.T, precision=highest
    )
    gram_block = (energy - mixed - mixed.T + curved) / entries
    cleaned = applied - jnp.dot(coefficients, basis_full, precision=highest) * inverse_root
    factor = jnp.linalg.cholesky(gram_block)
    new_block = lax.linalg.triangular_solve(factor, cleaned, left_side=True, lower=True)
    return (new_block, coefficients, factor)


def solution(mesh):
    return jax.shard_map(
        shards,
        mesh=mesh,
        in_specs=(
            P(None, ("row", "col")),
            P(),
            P(None, ("row", "col"), None, None),
            P(("row", "col")),
            P(("row", "col")),
        ),
        out_specs=(P(None, ("row", "col")), P(), P()),
        check_vma=False,
    )
```

profile of v0, /device:TPU:10, one launch (start us, length us, event | category | flops | bytes accessed | tf_op | source)
XLA Modules:
  0.0 118.9 jit_solution(17451722167365213223)
XLA Ops:
  7.2 0.7 compare_select_fusion
  7.9 0.7 compare_and_fusion
  8.6 1.0 convolution_convert_fusion
  9.6 11.2 %all_gather.3 = bf16[3,8,16384]{2,1,0:T(8,128)(2,1)S(1)} all-gather(bf16[3,8,4096]{2,1,0:T(8,128)(2,1)S(1)} %convolution_convert_fusion), channel_id=1, replica_groups=mesh['row'=4,'col'=8] {'row'}, dimensions={2}, use_global_device_ids=true | all-gather | bytes 983040 | tf_op jit(solution)/shard_map/all_gather | solution.py:20
  20.8 0.8 gather_fusion
  21.6 5.9 %fusion = f32[96,8,128,1]{2,1,3,0:T(8,128)S(1)} fusion(bf16[3,96,128,128]{3,2,1,0:T(8,128)(2,1)} %param.7, bf16[96,3,8,128]{3,2,1,0:T(8,128)(2,1)S(1)} %gather_fusion, pred[96]{0:T(512)(128)(4,1)S(1)} %compare_and_fusion), kind=kOutput, calls=%fused_computation.1 | convolution fusion | flops 75792384 | bytes 10420320 | tf_op jit(solution)/shard_map/mtij,mbtj->bti/dot_general | solution.py:23
  27.5 0.7 convolution_bitcast_fusion
  28.2 0.3 copy.13
  28.5 1.6 %copy.31 = f32[1,8,256,128]{3,1,2,0:T(8,128)} copy(f32[1,8,256,128]{3,2,1,0:T(8,128)S(1)} %bitcast.54) | data formatting | bytes 2097152
  30.2 0.2 convolution_multiply_fusion.1
  30.4 29.0 %reduce-scatter.2.cloned.1.call-done = f32[8,4096]{1,0:T(8,128)} async-done(((f32[8,32768]{1,0:T(8,128)}), f32[8,4096]{1,0:T(8,128)}) %reduce-scatter.2.cloned.1.call-update) | async-done | bytes 131088 | tf_op jit(solution)/shard_map/reduce_scatter | solution.py:31
  59.4 1.3 %convolution_multiply_fusion.2 = f32[8,40]{1,0:T(8,128)S(1)} fusion(f32[8,4096]{1,0:T(8,128)} %reduce-scatter.2.cloned.1.call-done, bf16[40,4096]{1,0:T(8,128)(2,1)S(1)} %copy-done), kind=kOutput, calls=%fused_computation.12 | convolution fusion | flops 15728960 | bytes 460032 | tf_op jit(solution)/shard_map/dot_general | solution.py:32
  60.7 1.3 %fusion.19 = f32[8,8]{0,1:T(8,128)S(1)} fusion(f32[8,4096]{1,0:T(8,128)} %reduce-scatter.2.cloned.1.call-done), kind=kOutput, calls=%fused_computation.39 | convolution fusion | flops 3145728 | bytes 131328 | tf_op jit(solution)/shard_map/dot_general | solution.py:34
  62.0 43.9 %all-reduce = (f32[8,40]{1,0:T(8,128)S(1)}, f32[40,40]{1,0:T(8,128)S(1)}, f32[8,8]{0,1:T(8,128)S(1)}) all-reduce(f32[8,40]{1,0:T(8,128)S(1)} %convolution_multiply_fusion.2, f32[40,40]{1,0:T(8,128)S(1)} %convolution_multiply_fusion.1, f32[8,8]{0,1:T(8,128)S(1)} %fusion.19), channel_id=1, replica_groups=mesh['row'=4,'col'=8] {'row','col'}, use_global_device_ids=true, to_apply=%region_2.3 | all-reduce | flops 1984 | bytes 15872 | tf_op jit(solution)/shard_map/psum | solution.py:35
  105.9 0.1 fusion.3
  106.0 0.1 fusion.20
  106.2 0.1 fusion.21
  106.4 0.1 fusion.4
  106.6 0.7 cholesky.16
  107.4 0.6 compare_reduce_fusion
  108.0 1.2 %select_bitcast_fusion = (f32[1,8,8]{2,1,0:T(8,128)S(1)}, f32[8,8]{1,0:T(8,128)}) fusion(f32[8,8]{1,0:T(8,128)S(1)} %cholesky.16, pred[]{:T(512)} %compare_reduce_fusion), kind=kLoop, calls=%fused_computation.30 | loop fusion | flops 256 | bytes 769 | tf_op jit(solution)/shard_map/triangular_solve | solution.py:45
  109.3 0.6 custom-call.6
  109.9 1.2 fusion.2
  111.1 1.0 fusion.15
  (13 shorter events, 0.3 us)
Async XLA Ops:
  7.2 1.4 %copy-start = (bf16[40,4096]{1,0:T(8,128)(2,1)S(1)}, bf16[40,4096]{1,0:T(8,128)(2,1)}, u32[]{:S(2)}) copy-start(bf16[40,4096]{1,0:T(8,128)(2,1)} %param.5) | copy-start | bytes 983044
  7.2 20.3 %copy-start.2 = (s32[96]{0:T(128)S(1)}, s32[96]{0:T(128)}, u32[]{:S(2)}) copy-start(s32[96]{0:T(128)} %param.8) | copy-start | bytes 1156
  7.2 52.2 %reduce-scatter.2.cloned.1.call-start = ((), (), s32[]{:S(2)}) async-start(), calls=%async_computation.1 | async-start | bytes 1179648 | tf_op jit(solution)/shard_map/reduce_scatter | solution.py:31
  106.0 6.0 %copy-start.1 = (f32[8,40]{1,0:T(8,128)}, f32[8,40]{1,0:T(8,128)S(1)}, u32[]{:S(2)}) copy-start(f32[8,40]{1,0:T(8,128)S(1)} %fusion.3) | copy-start | bytes 3844
Sparse Core Ops, SparseCore 0:
  30.3 29.0 reduce-scatter.1
where the time goes:
time: 119 us
  blocking collectives  55.1 us (46%)
  waiting for transfers between devices  29 us (24%)
  between operations  14.1 us (12%)
  matrix products  13.1 us (11%)
  other arithmetic  4.65 us (4%)
  local copies, waits for them, and re-layouts  2.88 us (2%)
    psum x1, blocking collectives, shards(): lax.psum((raw_proj, correlation, energy), ('row', 'col'))  43.9 us
    reduce_scatter x1, waiting for transfers between devices, shards(): lax.psum_scatter(partial_value, 'col', scatter_dimension=1, tiled=True)  29 us
    all_gather x1, blocking collectives, shards(): gathered = lax.all_gather(series, 'row', axis=2, tiled=True)  11.2 us
    dot_general x1, matrix products, shards(): jnp.einsum('mtij,mbtj->bti', tiles, picked, preferred_element_type=jnp.fl...  5.9 us
  transfers between devices with their start and end apart: 1, of which 1 were waited for; matrix products, arithmetic and copies ran while one was open for 0% of the time, Pallas kernels for 0%

commit v1 on v0

--- a/solution.py
+++ b/solution.py
@@ -17,7 +17,7 @@
     region = length // tile_size
     basis_full = basis.astype(jnp.float32)
     series = jnp.einsum("mbk,kn->mbn", expand, basis_full, precision=highest).astype(jnp.bfloat16)
-    gathered = lax.all_gather(series, "row", axis=2, tiled=True)
+    gathered = jnp.concatenate(lax.all_gather(series, "row"), axis=2)
     col_tiles = gathered.reshape(3, block_size, row_count * length // tile_size, tile_size)
     picked = jnp.take(col_tiles, tile_cols, axis=2)
     products = jnp.einsum("mtij,mbtj->bti", tiles, picked, preferred_element_type=jnp.float32)

time: 119 us -> 121 us (1.017)
  local copies, waits for them, and re-layouts: 2.88 us -> 4.81 us
    another operation x0 -> x2, local copies, waits for them, and re-layouts: none -> 1.32 us  [shards(): gathered.reshape(3, block_size, row_count * length // tile_size, tile_size)]
where the time goes in v1:
time: 121 us
  blocking collectives  55.1 us (46%)
  waiting for transfers between devices  29 us (24%)
  between operations  14.1 us (12%)
  matrix products  13.1 us (11%)
  local copies, waits for them, and re-layouts  4.81 us (4%)
  other arithmetic  4.65 us (4%)
    psum x1, blocking collectives, shards(): lax.psum((raw_proj, correlation, energy), ('row', 'col'))  43.9 us
    reduce_scatter x1, waiting for transfers between devices, shards(): lax.psum_scatter(partial_value, 'col', scatter_dimension=1, tiled=True)  29 us
    all_gather x1, blocking collectives, shards(): gathered = jnp.concatenate(lax.all_gather(series, 'row'), axis=2)  11.2 us
    dot_general x1, matrix products, shards(): jnp.einsum('mtij,mbtj->bti', tiles, picked, preferred_element_type=jnp.fl...  5.9 us
  transfers between devices with their start and end apart: 1, of which 1 were waited for; matrix products, arithmetic and copies ran while one was open for 0% of the time, Pallas kernels for 0%

profile of v1, /device:TPU:10, one launch (start us, length us, event | category | flops | bytes accessed | tf_op | source)
XLA Modules:
  0.0 120.9 jit_solution(13950900573527171333)
XLA Ops:
  7.2 0.7 compare_select_fusion
  7.9 0.7 compare_and_fusion
  8.6 1.0 convolution_convert_fusion
  9.6 11.2 %all-gather = bf16[12,8,4096]{2,1,0:T(8,128)(2,1)S(1)} all-gather(bf16[3,8,4096]{2,1,0:T(8,128)(2,1)S(1)} %convolution_convert_fusion), channel_id=2, replica_groups=mesh['row'=4,'col'=8] {'row'}, dimensions={0}, use_global_device_ids=true | all-gather | bytes 983040 | tf_op jit(solution)/shard_map/all_gather | solution.py:20
  20.8 0.6 copy.44
  21.4 0.8 reshape_reshape.3
  22.2 0.5 copy.22
  22.8 0.8 gather_fusion
  23.6 5.9 %fusion.3 = f32[8,96,128]{2,0,1:T(8,128)S(1)} fusion(bf16[3,96,128,128]{3,2,1,0:T(8,128)(2,1)} %param.7, bf16[96,3,8,128]{3,2,1,0:T(8,128)(2,1)S(1)} %gather_fusion, pred[96]{0:T(512)(128)(4,1)S(1)} %compare_and_fusion), kind=kOutput, calls=%fused_computation.7 | convolution fusion | flops 75792384 | bytes 10420320 | tf_op jit(solution)/shard_map/mtij,mbtj->bti/dot_general | solution.py:23
  29.5 0.7 convolution_bitcast_fusion
  30.2 0.3 copy.25
  30.5 1.6 %copy.43 = f32[1,8,256,128]{3,1,2,0:T(8,128)} copy(f32[1,8,256,128]{3,2,1,0:T(8,128)S(1)} %bitcast.57) | data formatting | bytes 2097152
  32.1 0.2 convolution_multiply_fusion.1
  32.3 29.0 %reduce-scatter.2.cloned.1.call-done = f32[8,4096]{1,0:T(8,128)} async-done(((f32[8,32768]{1,0:T(8,128)}), f32[8,4096]{1,0:T(8,128)}) %reduce-scatter.2.cloned.1.call-update) | async-done | bytes 131088 | tf_op jit(solution)/shard_map/reduce_scatter | solution.py:31
  61.3 1.3 %convolution_multiply_fusion.2 = f32[8,40]{1,0:T(8,128)S(1)} fusion(f32[8,4096]{1,0:T(8,128)} %reduce-scatter.2.cloned.1.call-done, bf16[40,4096]{1,0:T(8,128)(2,1)S(1)} %copy-done), kind=kOutput, calls=%fused_computation.13 | convolution fusion | flops 15728960 | bytes 460032 | tf_op jit(solution)/shard_map/dot_general | solution.py:32
  62.6 1.3 %fusion.21 = f32[8,8]{0,1:T(8,128)S(1)} fusion(f32[8,4096]{1,0:T(8,128)} %reduce-scatter.2.cloned.1.call-done), kind=kOutput, calls=%fused_computation.40 | convolution fusion | flops 3145728 | bytes 131328 | tf_op jit(solution)/shard_map/dot_general | solution.py:34
  63.9 43.9 %all-reduce = (f32[8,40]{1,0:T(8,128)S(1)}, f32[40,40]{1,0:T(8,128)S(1)}, f32[8,8]{0,1:T(8,128)S(1)}) all-reduce(f32[8,40]{1,0:T(8,128)S(1)} %convolution_multiply_fusion.2, f32[40,40]{1,0:T(8,128)S(1)} %convolution_multiply_fusion.1, f32[8,8]{0,1:T(8,128)S(1)} %fusion.21), channel_id=1, replica_groups=mesh['row'=4,'col'=8] {'row','col'}, use_global_device_ids=true, to_apply=%region_2.3 | all-reduce | flops 1984 | bytes 15872 | tf_op jit(solution)/shard_map/psum | solution.py:35
  108.4 0.1 fusion.7
  108.6 0.7 cholesky.16
  109.4 0.6 compare_reduce_fusion
  110.0 1.2 %select_bitcast_fusion = (f32[1,8,8]{2,1,0:T(8,128)S(1)}, f32[8,8]{1,0:T(8,128)}) fusion(f32[8,8]{1,0:T(8,128)S(1)} %cholesky.16, pred[]{:T(512)} %compare_reduce_fusion), kind=kLoop, calls=%fused_computation.31 | loop fusion | flops 256 | bytes 769 | tf_op jit(solution)/shard_map/triangular_solve | solution.py:45
  111.2 0.6 custom-call.6
  111.9 1.2 fusion.2
  113.0 1.0 fusion.17
  (16 shorter events, 0.7 us)
Async XLA Ops:
  7.2 1.4 %copy-start = (bf16[40,4096]{1,0:T(8,128)(2,1)S(1)}, bf16[40,4096]{1,0:T(8,128)(2,1)}, u32[]{:S(2)}) copy-start(bf16[40,4096]{1,0:T(8,128)(2,1)} %param.5) | copy-start | bytes 983044
  7.2 22.3 %copy-start.2 = (s32[96]{0:T(128)S(1)}, s32[96]{0:T(128)}, u32[]{:S(2)}) copy-start(s32[96]{0:T(128)} %param.8) | copy-start | bytes 1156
  7.2 54.1 %reduce-scatter.2.cloned.1.call-start = ((), (), s32[]{:S(2)}) async-start(), calls=%async_computation.1 | async-start | bytes 1179648 | tf_op jit(solution)/shard_map/reduce_scatter | solution.py:31
  108.0 6.0 %copy-start.1 = (f32[8,40]{1,0:T(8,128)}, f32[8,40]{1,0:T(8,128)S(1)}, u32[]{:S(2)}) copy-start(f32[8,40]{1,0:T(8,128)S(1)} %fusion.6) | copy-start | bytes 3844
Sparse Core Ops, SparseCore 0:
  32.2 29.0 reduce-scatter.1

commit v2 on v0

--- a/solution.py
+++ b/solution.py
@@ -32,7 +32,9 @@
     raw_proj = jnp.dot(applied, basis_full.T, precision=highest) * inverse_root
     correlation = jnp.dot(basis_full, basis_full.T, precision=highest) / entries
     energy = jnp.dot(applied, applied.T, precision=highest)
-    first_pass, correlation, energy = lax.psum((raw_proj, correlation, energy), ("row", "col"))
+    first_pass, correlation, energy = lax.psum(
+        lax.psum((raw_proj, correlation, energy), "col"), "row"
+    )
     second_pass = first_pass - jnp.dot(first_pass, correlation, precision=highest)
     coefficients = first_pass + second_pass
     mixed = jnp.dot(first_pass, coefficients.T, precision=highest)

time: 119 us -> 123 us (1.034)
  the two profiles are of different devices: /device:TPU:10 before, /device:TPU:0 now
where the time goes in v2:
time: 123 us
  blocking collectives  55.3 us (45%)
  waiting for transfers between devices  32.9 us (27%)
  between operations  14.1 us (11%)
  matrix products  13.1 us (11%)
  other arithmetic  4.65 us (4%)
  local copies, waits for them, and re-layouts  2.88 us (2%)
    reduce_scatter x1, waiting for transfers between devices, shards(): lax.psum_scatter(partial_value, 'col', scatter_dimension=1, tiled=True)  32.8 us
    psum x1, blocking collectives, shards(): lax.psum((raw_proj, correlation, energy), 'col')  26 us
    psum x1, blocking collectives, shards(): lax.psum(lax.psum((raw_proj, correlation, energy), 'col'), 'row')  16.6 us
    all_gather x1, blocking collectives, shards(): gathered = lax.all_gather(series, 'row', axis=2, tiled=True)  12.7 us
    dot_general x1, matrix products, shards(): jnp.einsum('mtij,mbtj->bti', tiles, picked, preferred_element_type=jnp.fl...  5.9 us
  transfers between devices with their start and end apart: 1, of which 1 were waited for; matrix products, arithmetic and copies ran while one was open for 0% of the time, Pallas kernels for 0%

profile of v2, /device:TPU:0, one launch (start us, length us, event | category | flops | bytes accessed | tf_op | source)
XLA Modules:
  0.0 123.0 jit_solution(13946684138139590406)
XLA Ops:
  7.2 0.7 compare_select_fusion
  7.9 0.7 compare_and_fusion
  8.6 1.0 convolution_convert_fusion
  9.6 12.7 %all_gather.3 = bf16[3,8,16384]{2,1,0:T(8,128)(2,1)S(1)} all-gather(bf16[3,8,4096]{2,1,0:T(8,128)(2,1)S(1)} %convolution_convert_fusion), channel_id=1, replica_groups=mesh['row'=4,'col'=8] {'row'}, dimensions={2}, use_global_device_ids=true | all-gather | bytes 983040 | tf_op jit(solution)/shard_map/all_gather | solution.py:20
  22.3 0.8 gather_fusion
  23.1 5.9 %fusion = f32[96,8,128,1]{2,1,3,0:T(8,128)S(1)} fusion(bf16[3,96,128,128]{3,2,1,0:T(8,128)(2,1)} %param.7, bf16[96,3,8,128]{3,2,1,0:T(8,128)(2,1)S(1)} %gather_fusion, pred[96]{0:T(512)(128)(4,1)S(1)} %compare_and_fusion), kind=kOutput, calls=%fused_computation.1 | convolution fusion | flops 75792384 | bytes 10420320 | tf_op jit(solution)/shard_map/mtij,mbtj->bti/dot_general | solution.py:23
  29.0 0.7 convolution_bitcast_fusion
  29.7 0.3 copy.13
  30.0 1.6 %copy.31 = f32[1,8,256,128]{3,1,2,0:T(8,128)} copy(f32[1,8,256,128]{3,2,1,0:T(8,128)S(1)} %bitcast.54) | data formatting | bytes 2097152
  31.6 0.2 convolution_multiply_fusion.1
  31.9 32.8 %reduce-scatter.2.cloned.1.call-done = f32[8,4096]{1,0:T(8,128)} async-done(((f32[8,32768]{1,0:T(8,128)}), f32[8,4096]{1,0:T(8,128)}) %reduce-scatter.2.cloned.1.call-update) | async-done | bytes 131088 | tf_op jit(solution)/shard_map/reduce_scatter | solution.py:31
  64.7 1.3 %convolution_multiply_fusion.2 = f32[8,40]{1,0:T(8,128)S(1)} fusion(f32[8,4096]{1,0:T(8,128)} %reduce-scatter.2.cloned.1.call-done, bf16[40,4096]{1,0:T(8,128)(2,1)S(1)} %copy-done), kind=kOutput, calls=%fused_computation.12 | convolution fusion | flops 15728960 | bytes 460032 | tf_op jit(solution)/shard_map/dot_general | solution.py:32
  66.0 1.3 %fusion.19 = f32[8,8]{0,1:T(8,128)S(1)} fusion(f32[8,4096]{1,0:T(8,128)} %reduce-scatter.2.cloned.1.call-done), kind=kOutput, calls=%fused_computation.39 | convolution fusion | flops 3145728 | bytes 131328 | tf_op jit(solution)/shard_map/dot_general | solution.py:34
  67.3 26.0 %all-reduce = (f32[8,40]{1,0:T(8,128)S(1)}, f32[40,40]{1,0:T(8,128)S(1)}, f32[8,8]{0,1:T(8,128)S(1)}) all-reduce(f32[8,40]{1,0:T(8,128)S(1)} %convolution_multiply_fusion.2, f32[40,40]{1,0:T(8,128)S(1)} %convolution_multiply_fusion.1, f32[8,8]{0,1:T(8,128)S(1)} %fusion.19), channel_id=1, replica_groups=mesh['row'=4,'col'=8] {'col'}, use_global_device_ids=true, to_apply=%region_3.4 | all-reduce | flops 1984 | bytes 15872 | tf_op jit(solution)/shard_map/psum | solution.py:36
  93.3 16.6 %all-reduce.1 = (f32[8,40]{1,0:T(8,128)S(1)}, f32[40,40]{1,0:T(8,128)S(1)}, f32[8,8]{0,1:T(8,128)S(1)}) all-reduce(f32[8,40]{1,0:T(8,128)S(1)} %get-tuple-element.3, f32[40,40]{1,0:T(8,128)S(1)} %get-tuple-element.4, f32[8,8]{0,1:T(8,128)S(1)} %get-tuple-element.5), channel_id=1, replica_groups=mesh['row'=4,'col'=8] {'row'}, use_global_device_ids=true, to_apply=%region_4.5 | all-reduce | flops 1984 | bytes 15872 | tf_op jit(solution)/shard_map/psum | solution.py:35
  110.1 0.1 fusion.20
  110.2 0.1 fusion.21
  110.5 0.1 fusion.4
  110.7 0.7 cholesky.16
  111.4 0.6 compare_reduce_fusion
  112.1 1.2 %select_bitcast_fusion = (f32[1,8,8]{2,1,0:T(8,128)S(1)}, f32[8,8]{1,0:T(8,128)}) fusion(f32[8,8]{1,0:T(8,128)S(1)} %cholesky.16, pred[]{:T(512)} %compare_reduce_fusion), kind=kLoop, calls=%fused_computation.30 | loop fusion | flops 256 | bytes 769 | tf_op jit(solution)/shard_map/triangular_solve | solution.py:47
  113.3 0.6 custom-call.6
  114.0 1.2 fusion.2
  115.1 1.0 fusion.15
  (14 shorter events, 0.4 us)
Async XLA Ops:
  7.2 1.4 %copy-start = (bf16[40,4096]{1,0:T(8,128)(2,1)S(1)}, bf16[40,4096]{1,0:T(8,128)(2,1)}, u32[]{:S(2)}) copy-start(bf16[40,4096]{1,0:T(8,128)(2,1)} %param.5) | copy-start | bytes 983044
  7.2 21.8 %copy-start.2 = (s32[96]{0:T(128)S(1)}, s32[96]{0:T(128)}, u32[]{:S(2)}) copy-start(s32[96]{0:T(128)} %param.8) | copy-start | bytes 1156
  7.2 57.5 %reduce-scatter.2.cloned.1.call-start = ((), (), s32[]{:S(2)}) async-start(), calls=%async_computation.1 | async-start | bytes 1179648 | tf_op jit(solution)/shard_map/reduce_scatter | solution.py:31
  110.1 6.0 %copy-start.1 = (f32[8,40]{1,0:T(8,128)}, f32[8,40]{1,0:T(8,128)S(1)}, u32[]{:S(2)}) copy-start(f32[8,40]{1,0:T(8,128)S(1)} %fusion.3) | copy-start | bytes 3844
Sparse Core Ops, SparseCore 0:
  31.8 32.8 reduce-scatter.1
